TPU v7x, 32 devices: a whole 2x2x4 slice. The times are simulated.
32 devices in a mesh: gx: 4 (over y, core), gy: 2 (over x), gz: 4 (over z).
Axes of the slice: x: 2, y: 2, z: 4, core: 2. Of those that a mesh axis runs over, the one named last changes fastest.
Arguments:
- tokens: bfloat16 [32, 6144], P('gy'), may hold values from -6 to 6
- route: int32 [32, 2], P('gy'), may hold values from 0 to 3, all different within a row; in each aligned block of 16 rows (0 to 15, 16 to 31, ...) at most 12 rows name the same one
- weight_q: int32 [32, 2], P('gy'), may hold values from 1 to 65535
- w_gate: bfloat16 [4, 6144, 16384], P('gx', 'gy', 'gz'), may hold values from -0.078125 to 0.078125
- w_up: bfloat16 [4, 6144, 16384], P('gx', 'gy', 'gz'), may hold values from -0.078125 to 0.078125
- w_down: bfloat16 [4, 16384, 6144], P('gx', 'gz', 'gy'), may hold values from -0.046875 to 0.046875
Outputs:
- mixed: bfloat16 [32, 6144], P('gy', ('gx', 'gz'))
Inputs may be any that keep to these rules, and one draw needn't show every extreme that they name: `route`: the 2 entries of a row are different; in each block of 16 rows owned by one index of gy no expert is named by more than 12 rows, a bound that some block reaches.
All inputs are finite; a program needn't handle non-finite values.
Results may differ from a plain program's by a relative error of at most 0.0049.
Values may be sent and summed in bfloat16 or wider, within the bound.
A program may use at most 256 MiB of HBM per device.

v0:
```python
import jax
import jax.numpy as jnp
from jax import lax
from jax.sharding import PartitionSpec as P

CAP = 12


def per_device(tokens, route, weight_q, w_gate, w_up, w_down):
    expert = lax.axis_index("gx")
    width_z = lax.axis_size("gz")
    owners = lax.axis_size("gy")
    hits = (route == expert).astype(jnp.int32)
    routed = jnp.sum(hits, axis=1)
    slot_index = jnp.cumsum(routed) - 1
    columns = jnp.arange(CAP, dtype=jnp.int32)
    placing = (slot_index[None, :] == columns[:, None]) & (routed[None, :] > 0)
    place_half = placing.astype(jnp.bfloat16)
    place_full = placing.astype(jnp.float32)
    outgoing = jnp.dot(place_half, tokens, preferred_element_type=jnp.float32).astype(jnp.bfloat16)
    weights_f = weight_q.astype(jnp.float32)
    shares = weights_f / jnp.sum(weights_f, axis=1, keepdims=True)
    token_gate = jnp.sum(hits.astype(jnp.float32) * shares, axis=1)
    slot_gate = jnp.dot(place_full, token_gate, precision=lax.Precision.HIGHEST)
    gate_slab, up_slab = (
        lax.all_to_all(w_gate[0], "gy", split_axis=1, concat_axis=0, tiled=True),
        lax.all_to_all(w_up[0], "gy", split_axis=1, concat_axis=0, tiled=True),
    )
    piece = lax.all_gather(outgoing, "gy", axis=0, tiled=True)
    gate = jnp.dot(piece, gate_slab, preferred_element_type=jnp.float32)
    upper = jnp.dot(piece, up_slab, preferred_element_type=jnp.float32)
    hidden = (jax.nn.silu(gate) * upper).astype(jnp.bfloat16)
    down_local = w_down[0]
    partial_value = jnp.dot(
        lax.all_gather(hidden, "gy", axis=1, tiled=True),
        down_local,
        preferred_element_type=jnp.float32,
    )
    portion = CAP // width_z
    column_width = partial_value.shape[1]
    blocks = partial_value.reshape(owners, width_z, portion, column_width)
    narrowed = lax.psum_scatter(blocks, "gz", scatter_dimension=1, tiled=True)
    arrived = lax.all_to_all(narrowed, "gy", split_axis=0, concat_axis=1, tiled=True)
    full = jnp.transpose(arrived[0], (1, 0, 2)).reshape(portion, owners * column_width)
    first = lax.axis_index("gz") * portion
    gate_part = lax.dynamic_slice_in_dim(slot_gate, first, portion, 0)
    place_part = lax.dynamic_slice_in_dim(place_full, first, portion, 0)
    weighted = gate_part[:, None] * full
    contribution = jnp.dot(place_part.T, weighted, precision=lax.Precision.HIGHEST)
    result = lax.psum_scatter(contribution, ("gx", "gz"), scatter_dimension=1, tiled=True)
    return result.astype(jnp.bfloat16)


def solution(mesh):
    in_specs = (
        P("gy", None),
        P("gy", None),
        P("gy", None),
        P("gx", "gy", "gz"),
        P("gx", "gy", "gz"),
        P("gx", "gz", "gy"),
    )
    out_specs = P("gy", ("gx", "gz"))
    return jax.shard_map(
        per_device, mesh=mesh, in_specs=in_specs, out_specs=out_specs, check_vma=False
    )
```

profile of v0, /device:TPU:0, one launch (start us, length us, event | category | flops | bytes accessed | tf_op | source)
XLA Modules:
  0.0 822.6 jit_solution(7426309213816833088)
XLA Ops:
  6.5 32.7 %copy.36 = bf16[1,3072,4096]{1,2,0:T(8,128)(2,1)} copy(bf16[1,3072,4096]{2,1,0:T(8,128)(2,1)} %param.9) | data formatting | bytes 50331648 | tf_op args[3]
  39.2 11.8 %all-to-all-start = ((bf16[3072,2,2048]{0,2,1:T(8,128)(2,1)}), bf16[3072,2,2048]{0,2,1:T(8,128)(2,1)}, u32[]{:S(2)}, u32[]{:S(2)}) async-start(bf16[3072,2,2048]{0,2,1:T(8,128)(2,1)} %bitcast.37), calls=%async_computation | async-start | bytes 50331648 | tf_op jit(solution)/shard_map/all_to_all | solution.py:26
  51.0 32.7 %copy.38 = bf16[1,3072,4096]{1,2,0:T(8,128)(2,1)} copy(bf16[1,3072,4096]{2,1,0:T(8,128)(2,1)} %param.10) | data formatting | bytes 50331648 | tf_op args[4]
  83.7 240.8 %all-to-all-done = bf16[3072,2,2048]{0,2,1:T(8,128)(2,1)} async-done(((bf16[3072,2,2048]{0,2,1:T(8,128)(2,1)}), bf16[3072,2,2048]{0,2,1:T(8,128)(2,1)}, u32[]{:S(2)}, u32[]{:S(2)}) %all-to-all-start) | async-done | bytes 25165856 | tf_op jit(solution)/shard_map/all_to_all | solution.py:26
  324.5 11.9 %all-to-all-start.1 = ((bf16[3072,2,2048]{0,2,1:T(8,128)(2,1)}), bf16[3072,2,2048]{0,2,1:T(8,128)(2,1)}, u32[]{:S(2)}, u32[]{:S(2)}) async-start(bf16[3072,2,2048]{0,2,1:T(8,128)(2,1)} %bitcast.36), calls=%async_computation.1 | async-start | bytes 50331648 | tf_op jit(solution)/shard_map/all_to_all | solution.py:27
  336.5 0.0 all-reduce.3.cloned.1.call-start
  336.6 0.1 copy.35
  336.7 0.1 add_reduce_fusion
  336.8 0.2 fusion.2
  337.0 275.4 %all-gather = bf16[2,12,6144]{2,1,0:T(8,128)(2,1)S(1)} all-gather(bf16[1,12,6144]{2,1,0:T(8,128)(2,1)S(1)} %fusion.2), channel_id=1, replica_groups=mesh['gx'=4,'gy'=2,'gz'=4] {'gy'}, dimensions={0}, use_global_device_ids=true | all-gather | bytes 442368 | tf_op jit(solution)/shard_map/all_gather | solution.py:29
  612.4 0.1 reshape.53
  612.5 0.6 dynamic-slice
  613.1 31.6 %copy.37 = bf16[2,3072,2048]{2,1,0:T(8,128)(2,1)} copy(bf16[2,3072,2048]{1,2,0:T(8,128)(2,1)} %bitcast.5) | data formatting | bytes 50331648 | tf_op jit(solution)/shard_map/all_to_all | solution.py:26
  644.7 32.7 %copy.39 = bf16[2,3072,2048]{2,1,0:T(8,128)(2,1)} copy(bf16[2,3072,2048]{1,2,0:T(8,128)(2,1)} %bitcast.8) | data formatting | bytes 50331648 | tf_op jit(solution)/shard_map/all_to_all | solution.py:27
  677.4 9.9 %fusion.16 = f32[24,2048]{1,0:T(8,128)S(1)} fusion(bf16[24,6144]{1,0:T(8,128)(2,1)S(1)} %reshape.53, bf16[6144,2048]{1,0:T(8,128)(2,1)} %bitcast.34), kind=kOutput, calls=%fused_computation.25 | convolution fusion | flops 603979776 | bytes 25657344 | tf_op jit(solution)/shard_map/dot_general | solution.py:30
  687.3 10.0 %fusion.3 = bf16[24,2048]{1,0:T(8,128)(2,1)S(1)} fusion(bf16[24,6144]{1,0:T(8,128)(2,1)S(1)} %reshape.53, bf16[6144,2048]{1,0:T(8,128)(2,1)} %bitcast.35, f32[24,2048]{1,0:T(8,128)S(1)} %fusion.16), kind=kOutput, calls=%fused_computation.5 | convolution fusion | flops 604274688 | bytes 25755648 | tf_op jit(solution)/shard_map/dot_general | solution.py:31
  697.3 5.3 all_gather.7
  702.6 0.1 dot_general.24
  702.8 11.3 %fusion = f32[2,4,3,3072]{3,0,2,1:T(2,128)} fusion(bf16[1,4096,3072]{2,1,0:T(8,128)(2,1)} %param.11, bf16[2,4,3,4096]{3,2,1,0:T(4,128)(2,1)S(1)} %dot_general.24), kind=kOutput, calls=%fused_computation | convolution fusion | flops 603979776 | bytes 25657344 | tf_op jit(solution)/shard_map/dot_general | solution.py:34
  714.1 0.0 all-reduce.3.cloned.1.call-update
  714.1 36.5 %all-reduce.3.cloned.1.call-done = f32[2,4,3,3072]{3,0,2,1:T(2,128)} async-done(((f32[2,4,3,3072]{3,0,2,1:T(2,128)}), f32[2,4,3,3072]{3,0,2,1:T(2,128)}) %all-reduce.3.cloned.1.call-update) | async-done | bytes 294928
  750.6 1.5 constant_dynamic-slice_fusion
  752.1 0.7 copy.42
  752.8 3.3 all-to-all-start.2
  756.1 0.0 reduce-scatter.2.cloned.1.call-start
  756.2 0.1 convolution_bitcast_fusion
  756.3 0.1 dynamic_slice.7
  756.4 3.9 all-to-all-done.2
  760.4 1.2 fusion.5
  761.6 0.0 reduce-scatter.2.cloned.1.call-update
  761.6 52.8 %reduce-scatter.2.cloned.1.call-done = f32[16,384]{1,0:T(8,128)} async-done(((f32[16,6144]{1,0:T(8,128)}), f32[16,384]{1,0:T(8,128)}) %reduce-scatter.2.cloned.1.call-update) | async-done | bytes 24592 | tf_op jit(solution)/shard_map/reduce_scatter | solution.py:50
  814.4 1.3 convert_element_type.25
  (19 shorter events, 0.2 us)
Async XLA Ops:
  6.5 330.3 %copy-start = (bf16[16,6144]{1,0:T(8,128)(2,1)S(1)}, bf16[16,6144]{1,0:T(8,128)(2,1)}, u32[]{:S(2)}) copy-start(bf16[16,6144]{1,0:T(8,128)(2,1)} %param.6) | copy-start | bytes 589828
  39.2 285.3 %all-to-all-start = ((bf16[3072,2,2048]{0,2,1:T(8,128)(2,1)}), bf16[3072,2,2048]{0,2,1:T(8,128)(2,1)}, u32[]{:S(2)}, u32[]{:S(2)}) async-start(bf16[3072,2,2048]{0,2,1:T(8,128)(2,1)} %bitcast.37), calls=%async_computation | async-start | bytes 50331648 | tf_op jit(solution)/shard_map/all_to_all | solution.py:26
  324.5 12.0 %copy-start.2 = (s32[16,2]{0,1:T(2,128)S(1)}, s32[16,2]{0,1:T(2,128)}, u32[]{:S(2)}) copy-start(s32[16,2]{0,1:T(2,128)} %param.7) | copy-start | bytes 388
  324.5 288.0 %copy-start.4 = (u32[32]{0:T(128)S(1)}, u32[32]{0:T(128)}, u32[]{:S(2)}) copy-start(u32[32]{0:T(128)} %constant.30) | copy-start | bytes 388
  324.5 288.5 %copy-start.3 = (s32[16,2]{0,1:T(2,128)S(1)}, s32[16,2]{0,1:T(2,128)}, u32[]{:S(2)}) copy-start(s32[16,2]{0,1:T(2,128)} %param.8) | copy-start | bytes 388
  324.5 320.2 %all-to-all-start.1 = ((bf16[3072,2,2048]{0,2,1:T(8,128)(2,1)}), bf16[3072,2,2048]{0,2,1:T(8,128)(2,1)}, u32[]{:S(2)}, u32[]{:S(2)}) async-start(bf16[3072,2,2048]{0,2,1:T(8,128)(2,1)} %bitcast.36), calls=%async_computation.1 | async-start | bytes 50331648 | tf_op jit(solution)/shard_map/all_to_all | solution.py:27
  336.5 414.1 %all-reduce.3.cloned.1.call-start = ((), (), s32[]{:S(2)}) async-start(), calls=%async_computation.5 | async-start | bytes 589824
  687.3 128.5 %copy-start.1 = (bf16[16,6144]{1,0:T(8,128)(2,1)S(1)}, bf16[16,6144]{1,0:T(8,128)(2,1)}, u32[]{:S(2)}) copy-start(bf16[16,6144]{1,0:T(8,128)(2,1)} %param.6) | copy-start | bytes 589828
  752.8 7.5 all-to-all-start.2
  756.1 58.3 %reduce-scatter.2.cloned.1.call-start = ((), (), s32[]{:S(2)}) async-start(), calls=%async_computation.4 | async-start | bytes 417792 | tf_op jit(solution)/shard_map/reduce_scatter | solution.py:50
Sparse Core Ops, SparseCore 0:
  714.2 36.3 all-reduce.2
  761.7 52.6 reduce-scatter.1
where the time goes:
time: 826 us; the launch traced here: 823 us
  waiting for transfers between devices  334 us (40%)
  blocking collectives  281 us (34%)
  local copies, waits for them, and re-layouts  133 us (16%)
  matrix products  32.7 us (4%)
  starting transfers between devices  27.1 us (3%)
  between operations  13.5 us (2%)
    all_gather x1, blocking collectives, per_device(): piece = lax.all_gather(outgoing, 'gy', axis=0, tiled=True)  275 us
    all_to_all x1, waiting for transfers between devices, per_device(): lax.all_to_all(w_gate[0], 'gy', split_axis=1, concat_axis=0, tiled=True)  241 us
    unnamed x16, local copies, waits for them, and re-layouts  67.6 us
    reduce_scatter x1, waiting for transfers between devices, per_device(): lax.psum_scatter(contribution, ('gx', 'gz'), scatter_dimension=1, tiled=T...  52.8 us
    unnamed x3, waiting for transfers between devices  36.5 us
    all_to_all x1, local copies, waits for them, and re-layouts, per_device(): lax.all_to_all(w_up[0], 'gy', split_axis=1, concat_axis=0, tiled=True)  32.7 us
    all_to_all x1, local copies, waits for them, and re-layouts, per_device(): lax.all_to_all(w_gate[0], 'gy', split_axis=1, concat_axis=0, tiled=True)  31.6 us
  transfers between devices with their start and end apart: 5, of which 4 were waited for; matrix products, arithmetic and copies ran while one was open for 8% of the time, Pallas kernels for 0%

commit v1 on v0

--- a/solution.py
+++ b/solution.py
@@ -23,7 +23,12 @@
     token_gate = jnp.sum(hits.astype(jnp.float32) * shares, axis=1)
     slot_gate = jnp.dot(place_full, token_gate, precision=lax.Precision.HIGHEST)
     gate_slab, up_slab = (
-        lax.all_to_all(w_gate[0], "gy", split_axis=1, concat_axis=0, tiled=True),
+        jnp.concatenate(
+            lax.all_to_all(
+                jnp.stack(jnp.split(w_gate[0], lax.axis_size("gy"), axis=1)), "gy", 0, 0
+            ),
+            axis=0,
+        ),
         lax.all_to_all(w_up[0], "gy", split_axis=1, concat_axis=0, tiled=True),
     )
     piece = lax.all_gather(outgoing, "gy", axis=0, tiled=True)

time: 826 us -> 792 us (0.959)
  local copies, waits for them, and re-layouts: 133 us -> 77.5 us
  waiting for transfers between devices: 334 us -> 347 us
  other arithmetic: 1.57 us -> 11.6 us
    all_to_all x1, waiting for transfers between devices: 0.01 us -> 254 us  [per_device(): lax.all_to_all(w_up[0], 'gy', split_axis=1, concat_axis=0, tiled=True)]
    all_to_all x1, waiting for transfers between devices: 241 us -> 0.01 us  [per_device(): lax.all_to_all(jnp.stack(jnp.split(w_gate[0], lax.axis_size('gy'), axis=1...]
    unnamed x16 -> x13, local copies, waits for them, and re-layouts: 67.6 us -> 35 us
    all_to_all x1 -> x0, local copies, waits for them, and re-layouts: 31.6 us -> none  [per_device(): lax.all_to_all(w_gate[0], 'gy', split_axis=1, concat_axis=0, tiled=True)]
    another operation x1 -> x2, other arithmetic: 0.04 us -> 10.1 us  [the longest x1 10 us: per_device(): jnp.stack(jnp.split(w_gate[0], lax.axis_size('gy'), axis=1))]
    another operation x1 -> x2, local copies, waits for them, and re-layouts: 0.09 us -> 10 us  [the longest x1 9.91 us: per_device(): jnp.stack(jnp.split(w_gate[0], lax.axis_size('gy'), axis=1))]
  transfers between devices with their start and end apart: 5 -> 5, of which waited for: 4 -> 4; matrix products, arithmetic and copies ran while one was open for 8% -> 7% of each run, Pallas kernels for 0% -> 0%
where the time goes in v1:
time: 792 us; the launch traced here: 790 us
  waiting for transfers between devices  347 us (44%)
  blocking collectives  281 us (35%)
  local copies, waits for them, and re-layouts  77.5 us (10%)
  matrix products  32.7 us (4%)
  starting transfers between devices  26.9 us (3%)
  between operations  13.5 us (2%)
  other arithmetic  11.6 us (1%)
    all_gather x1, blocking collectives, per_device(): piece = lax.all_gather(outgoing, 'gy', axis=0, tiled=True)  275 us
    all_to_all x1, waiting for transfers between devices, per_device(): lax.all_to_all(w_up[0], 'gy', split_axis=1, concat_axis=0, tiled=True)  254 us
    reduce_scatter x1, waiting for transfers between devices, per_device(): lax.psum_scatter(contribution, ('gx', 'gz'), scatter_dimension=1, tiled=T...  52.9 us
    unnamed x3, waiting for transfers between devices  36.5 us
    unnamed x13, local copies, waits for them, and re-layouts  35 us
    all_to_all x1, local copies, waits for them, and re-layouts, per_device(): lax.all_to_all(w_up[0], 'gy', split_axis=1, concat_axis=0, tiled=True)  31.6 us
  transfers between devices with their start and end apart: 5, of which 4 were waited for; matrix products, arithmetic and copies ran while one was open for 7% of the time, Pallas kernels for 0%

profile of v1, /device:TPU:0, one launch (start us, length us, event | category | flops | bytes accessed | tf_op | source)
XLA Modules:
  0.0 789.7 jit_solution(18056481269653233885)
XLA Ops:
  6.5 32.7 %copy.30 = bf16[1,3072,4096]{1,2,0:T(8,128)(2,1)} copy(bf16[1,3072,4096]{2,1,0:T(8,128)(2,1)} %param.10) | data formatting | bytes 50331648 | tf_op args[4]
  39.3 11.8 %all-to-all-start.1 = ((bf16[3072,2,2048]{0,2,1:T(8,128)(2,1)}), bf16[3072,2,2048]{0,2,1:T(8,128)(2,1)}, u32[]{:S(2)}, u32[]{:S(2)}) async-start(bf16[3072,2,2048]{0,2,1:T(8,128)(2,1)} %bitcast.38), calls=%async_computation.1 | async-start | bytes 50331648 | tf_op jit(solution)/shard_map/all_to_all | solution.py:32
  51.1 9.9 %slice_bitcast_fusion.1 = (bf16[1,3072,2048]{2,1,0:T(8,128)(2,1)S(1)}, bf16[1,3072,2048]{2,1,0:T(8,128)(2,1)S(1)}) fusion(bf16[3072,4096]{1,0:T(8,128)(2,1)} %bitcast.39), kind=kLoop, calls=%fused_computation.4 | loop fusion | bytes 50331648 | tf_op jit(solution)/shard_map/stack | solution.py:28
  61.0 10.0 %pad_maximum_fusion = bf16[2,3072,2048]{2,1,0:T(8,128)(2,1)} fusion(bf16[1,3072,2048]{2,1,0:T(8,128)(2,1)S(1)} %get-tuple-element.6, bf16[1,3072,2048]{2,1,0:T(8,128)(2,1)S(1)} %get-tuple-element.5), kind=kLoop, calls=%fused_computation | loop fusion | flops 12582912 | bytes 50331648 | tf_op jit(solution)/shard_map/stack | solution.py:28
  71.0 253.6 %all-to-all-done.1 = bf16[3072,2,2048]{0,2,1:T(8,128)(2,1)} async-done(((bf16[3072,2,2048]{0,2,1:T(8,128)(2,1)}), bf16[3072,2,2048]{0,2,1:T(8,128)(2,1)}, u32[]{:S(2)}, u32[]{:S(2)}) %all-to-all-start.1) | async-done | bytes 25165856 | tf_op jit(solution)/shard_map/all_to_all | solution.py:32
  324.6 11.7 %all-to-all-start = ((bf16[2,3072,2048]{2,1,0:T(8,128)(2,1)}), bf16[2,3072,2048]{2,1,0:T(8,128)(2,1)}, u32[]{:S(2)}, u32[]{:S(2)}) async-start(bf16[2,3072,2048]{2,1,0:T(8,128)(2,1)} %pad_maximum_fusion), calls=%async_computation | async-start | bytes 50331648 | tf_op jit(solution)/shard_map/all_to_all | solution.py:27
  336.3 0.0 all-reduce.3.cloned.1.call-start
  336.4 0.1 copy.29
  336.5 0.1 add_reduce_fusion
  336.7 0.2 fusion.2
  336.9 275.4 %all-gather = bf16[2,12,6144]{2,1,0:T(8,128)(2,1)S(1)} all-gather(bf16[1,12,6144]{2,1,0:T(8,128)(2,1)S(1)} %fusion.2), channel_id=1, replica_groups=mesh['gx'=4,'gy'=2,'gz'=4] {'gy'}, dimensions={0}, use_global_device_ids=true | all-gather | bytes 442368 | tf_op jit(solution)/shard_map/all_gather | solution.py:34
  612.2 0.1 reshape.53
  612.3 0.6 dynamic-slice
  612.9 31.6 %copy.31 = bf16[2,3072,2048]{2,1,0:T(8,128)(2,1)} copy(bf16[2,3072,2048]{1,2,0:T(8,128)(2,1)} %bitcast.9) | data formatting | bytes 50331648 | tf_op jit(solution)/shard_map/all_to_all | solution.py:32
  644.5 9.9 %fusion.16 = f32[24,2048]{1,0:T(8,128)S(1)} fusion(bf16[24,6144]{1,0:T(8,128)(2,1)S(1)} %reshape.53, bf16[6144,2048]{1,0:T(8,128)(2,1)} %bitcast.7), kind=kOutput, calls=%fused_computation.28 | convolution fusion | flops 603979776 | bytes 25657344 | tf_op jit(solution)/shard_map/dot_general | solution.py:35
  654.4 10.0 %fusion.3 = bf16[24,2048]{1,0:T(8,128)(2,1)S(1)} fusion(bf16[24,6144]{1,0:T(8,128)(2,1)S(1)} %reshape.53, bf16[6144,2048]{1,0:T(8,128)(2,1)} %bitcast.37, f32[24,2048]{1,0:T(8,128)S(1)} %fusion.16), kind=kOutput, calls=%fused_computation.8 | convolution fusion | flops 604274688 | bytes 25755648 | tf_op jit(solution)/shard_map/dot_general | solution.py:36
  664.4 5.3 all_gather.7
  669.7 0.1 dot_general.24
  669.8 11.3 %fusion = f32[2,4,3,3072]{3,0,2,1:T(2,128)} fusion(bf16[1,4096,3072]{2,1,0:T(8,128)(2,1)} %param.11, bf16[2,4,3,4096]{3,2,1,0:T(4,128)(2,1)S(1)} %dot_general.24), kind=kOutput, calls=%fused_computation.1 | convolution fusion | flops 603979776 | bytes 25657344 | tf_op jit(solution)/shard_map/dot_general | solution.py:39
  681.1 0.0 all-reduce.3.cloned.1.call-update
  681.2 36.5 %all-reduce.3.cloned.1.call-done = f32[2,4,3,3072]{3,0,2,1:T(2,128)} async-done(((f32[2,4,3,3072]{3,0,2,1:T(2,128)}), f32[2,4,3,3072]{3,0,2,1:T(2,128)}) %all-reduce.3.cloned.1.call-update) | async-done | bytes 294928
  717.6 1.5 constant_dynamic-slice_fusion
  719.2 0.7 copy.34
  719.9 3.3 all-to-all-start.2
  723.2 0.0 reduce-scatter.2.cloned.1.call-start
  723.2 0.1 convolution_bitcast_fusion
  723.4 0.1 dynamic_slice.7
  723.4 3.9 all-to-all-done.2
  727.4 1.2 fusion.5
  728.6 0.0 reduce-scatter.2.cloned.1.call-update
  728.6 52.9 %reduce-scatter.2.cloned.1.call-done = f32[16,384]{1,0:T(8,128)} async-done(((f32[16,6144]{1,0:T(8,128)}), f32[16,384]{1,0:T(8,128)}) %reduce-scatter.2.cloned.1.call-update) | async-done | bytes 24592 | tf_op jit(solution)/shard_map/reduce_scatter | solution.py:55
  781.5 1.3 convert_element_type.25
  (17 shorter events, 0.2 us)
Async XLA Ops:
  6.5 330.1 %copy-start = (bf16[16,6144]{1,0:T(8,128)(2,1)S(1)}, bf16[16,6144]{1,0:T(8,128)(2,1)}, u32[]{:S(2)}) copy-start(bf16[16,6144]{1,0:T(8,128)(2,1)} %param.6) | copy-start | bytes 589828
  39.3 285.3 %all-to-all-start.1 = ((bf16[3072,2,2048]{0,2,1:T(8,128)(2,1)}), bf16[3072,2,2048]{0,2,1:T(8,128)(2,1)}, u32[]{:S(2)}, u32[]{:S(2)}) async-start(bf16[3072,2,2048]{0,2,1:T(8,128)(2,1)} %bitcast.38), calls=%async_computation.1 | async-start | bytes 50331648 | tf_op jit(solution)/shard_map/all_to_all | solution.py:32
  71.0 265.4 %copy-start.1 = (s32[16,2]{0,1:T(2,128)S(1)}, s32[16,2]{0,1:T(2,128)}, u32[]{:S(2)}) copy-start(s32[16,2]{0,1:T(2,128)} %param.7) | copy-start | bytes 388
  71.0 541.3 %copy-start.3 = (u32[32]{0:T(128)S(1)}, u32[32]{0:T(128)}, u32[]{:S(2)}) copy-start(u32[32]{0:T(128)} %constant.30) | copy-start | bytes 388
  71.0 541.9 %copy-start.2 = (s32[16,2]{0,1:T(2,128)S(1)}, s32[16,2]{0,1:T(2,128)}, u32[]{:S(2)}) copy-start(s32[16,2]{0,1:T(2,128)} %param.8) | copy-start | bytes 388
  324.6 319.9 %all-to-all-start = ((bf16[2,3072,2048]{2,1,0:T(8,128)(2,1)}), bf16[2,3072,2048]{2,1,0:T(8,128)(2,1)}, u32[]{:S(2)}, u32[]{:S(2)}) async-start(bf16[2,3072,2048]{2,1,0:T(8,128)(2,1)} %pad_maximum_fusion), calls=%async_computation | async-start | bytes 50331648 | tf_op jit(solution)/shard_map/all_to_all | solution.py:27
  336.3 381.3 %all-reduce.3.cloned.1.call-start = ((), (), s32[]{:S(2)}) async-start(), calls=%async_computation.5 | async-start | bytes 589824
  719.9 7.5 all-to-all-start.2
  723.2 58.3 %reduce-scatter.2.cloned.1.call-start = ((), (), s32[]{:S(2)}) async-start(), calls=%async_computation.4 | async-start | bytes 417792 | tf_op jit(solution)/shard_map/reduce_scatter | solution.py:55
Sparse Core Ops, SparseCore 0:
  681.3 36.3 all-reduce.2
  728.7 52.7 reduce-scatter.1
